TPU v7x, 32 devices: a whole 2x2x4 slice. The times are simulated.
32 devices in a mesh: gx: 8 (over z, x), gy: 4 (over y, core).
Axes of the slice: x: 2, y: 2, z: 4, core: 2. Of those that a mesh axis runs over, the one named last changes fastest.
Arguments:
- populations: float32 [19, 48, 32, 128], P(None, 'gx', 'gy'), may hold values from 0.03 to 0.06
- cell_mass: float32 [48, 32, 128], P('gx', 'gy'), may hold values from 0.05 to 1
- cell_flags: int32 [48, 32, 128], P('gx', 'gy'), may hold values from 0 to 2
- bubble: int32 [48, 32, 128], P('gx', 'gy'), may hold values from 0 to 95, as said below
- conversion: int32 [48, 32, 128], P('gx', 'gy'), may hold values 0 or 1
- rest_volume: float32 [96], replicated, may hold values from 256 to 2048
Outputs:
- relaxed_populations: float32 [19, 48, 32, 128], P(None, 'gx', 'gy')
- new_mass: float32 [48, 32, 128], P('gx', 'gy')
- gas_density: float32 [96], replicated
Inputs may be any that keep to these rules, and one draw needn't show every extreme that they name: `cell_flags`: 0 gas, 1 interface, 2 liquid. The bubble that a gas or interface cell belongs to; unused for liquid cells. `conversion`: 1 marks an interface cell that becomes liquid in this step; unused for other cells.
All inputs are finite; a program needn't handle non-finite values. No bound on the sum of `conversion` on one device may be relied on, other than what follows from the above.
Results may differ from a plain program's by a relative error of at most 0.0003.
Values sent between devices are 32-bit elements; how exact they have to be, the bound alone decides.
No kernel may reach another device: no remote copies, remote signals or barrier semaphores. Data moves between devices by JAX's collectives and lax.ppermute only.
A program may use at most 64 MiB of HBM per device.

v0:
```python
import jax
import jax.numpy as jnp
import numpy as np
from jax import lax
from jax.sharding import PartitionSpec as P

VELOCITIES = np.array(
    [
        [0, 0, 0],
        [1, 0, 0],
        [-1, 0, 0],
        [0, 1, 0],
        [0, -1, 0],
        [0, 0, 1],
        [0, 0, -1],
        [1, 1, 0],
        [-1, -1, 0],
        [1, -1, 0],
        [-1, 1, 0],
        [1, 0, 1],
        [-1, 0, -1],
        [1, 0, -1],
        [-1, 0, 1],
        [0, 1, 1],
        [0, -1, -1],
        [0, 1, -1],
        [0, -1, 1],
    ]
)
OPPOSITE = np.array([0, 2, 1, 4, 3, 6, 5, 8, 7, 10, 9, 12, 11, 14, 13, 16, 15, 18, 17])
WEIGHTS = np.array([1.0 / 3.0] + [1.0 / 18.0] * 6 + [1.0 / 36.0] * 12)
RELAX = 1.0 / 0.6
AMBIENT = 2.0


def padded_2(cells, sides, width):
    for axis, dim in sides:
        count = lax.axis_size(axis)
        ends = count - 1
        head = lax.slice_in_dim(cells, 0, width, axis=dim)
        tail = lax.slice_in_dim(cells, cells.shape[dim] - width, cells.shape[dim], axis=dim)
        cells = jnp.concatenate(
            [
                lax.ppermute(tail, axis, [(i, (i + 1) % count) for i in range(ends)]),
                cells,
                lax.ppermute(head, axis, [((i + 1) % count, i) for i in range(ends)]),
            ],
            axis=dim,
        )
    return cells


def moments(populations):
    density = jnp.sum(populations, axis=0)
    lattice = jnp.asarray(VELOCITIES.T, jnp.float32)
    flux = jnp.einsum("kq,qxyz->kxyz", lattice, populations, precision=lax.Precision.HIGHEST)
    return (density, flux / density[None])


def unit_equilibrium(velocity):
    lattice = jnp.asarray(VELOCITIES, jnp.float32)
    project = jnp.einsum("qk,kxyz->qxyz", lattice, velocity, precision=lax.Precision.HIGHEST)
    speed = jnp.sum(velocity * velocity, axis=0)
    weights = jnp.asarray(WEIGHTS, jnp.float32)[:, None, None, None]
    return weights * (1.0 + 3.0 * project + 4.5 * project * project - 1.5 * speed[None])


def window(layer, lane, extent_rows, extent_cols):
    offset_rows, offset_cols, offset_depth = (int(value) for value in VELOCITIES[lane])
    begin_rows, begin_cols = (1 - offset_rows, 1 - offset_cols)
    return jnp.roll(
        layer[begin_rows : begin_rows + extent_rows, begin_cols : begin_cols + extent_cols],
        offset_depth,
        axis=2,
    )


def domain(inside_rows, inside_cols, lane, extent_rows, extent_cols):
    begin_rows, begin_cols = (1 - int(VELOCITIES[lane][0]), 1 - int(VELOCITIES[lane][1]))
    return (
        inside_rows[begin_rows : begin_rows + extent_rows][:, None, None]
        & inside_cols[begin_cols : begin_cols + extent_cols][None, :, None]
    )


def pull_cells(padded, inside_rows, inside_cols, populations, fraction):
    extent_rows, extent_cols = (populations.shape[1], populations.shape[2])
    pulled = [populations[0]]
    gas_side = [jnp.zeros(populations.shape[1:], jnp.bool_)]
    mass_flux = jnp.zeros(populations.shape[1:], jnp.float32)
    targets = jnp.zeros(populations.shape[1:], jnp.float32)
    for lane in range(1, 19):
        source = window(padded[lane], lane, extent_rows, extent_cols)
        source_fraction = window(padded[19], lane, extent_rows, extent_cols)
        source_status = window(padded[20], lane, extent_rows, extent_cols)
        in_domain = domain(inside_rows, inside_cols, lane, extent_rows, extent_cols)
        source_flag = jnp.where(source_status > 2.5, source_status - 3.0, source_status)
        bounced = populations[int(OPPOSITE[lane])]
        pulled.append(jnp.where(in_domain, source, bounced))
        gas_side.append(in_domain & (source_flag < 0.5))
        weight = jnp.where(
            in_domain & (source_flag > 1.5),
            1.0,
            jnp.where(in_domain & (source_flag > 0.5), 0.5 * (fraction + source_fraction), 0.0),
        )
        mass_flux = mass_flux + weight * (source - bounced)
        targets = targets + jnp.where(in_domain & (jnp.abs(source_status - 1.0) < 0.5), 1.0, 0.0)
    return (jnp.stack(pulled), jnp.stack(gas_side), mass_flux, targets)


def settle_cells(
    pulled,
    gas_side,
    populations,
    velocity,
    local_gas,
    cell_mass,
    cell_flags,
    conversion,
    mass_flux,
    targets,
):
    unit = unit_equilibrium(velocity)
    paired = unit + unit[OPPOSITE]
    bounced = populations[OPPOSITE]
    wetted = cell_flags > 0
    passed = jnp.where(gas_side, local_gas[None] * paired - bounced, pulled)
    passed = jnp.where(wetted[None], passed, populations)
    moved_density, moved_velocity = moments(passed)
    relaxed = passed - RELAX * (passed - moved_density[None] * unit_equilibrium(moved_velocity))
    relaxed = jnp.where(wetted[None], relaxed, populations)
    filling = (cell_flags == 1) & (conversion == 1)
    updated = jnp.where(
        cell_flags == 1, cell_mass + mass_flux, jnp.where(cell_flags == 2, moved_density, cell_mass)
    )
    portion = jnp.where(filling, (updated - moved_density) / jnp.maximum(targets, 1.0), 0.0)
    updated = jnp.where(filling, moved_density, updated)
    return (relaxed, updated, portion)


def collect_spill(padded_portion, extent_rows, extent_cols):
    gained = jnp.zeros((extent_rows, extent_cols, padded_portion.shape[2]), jnp.float32)
    for lane in range(1, 19):
        gained = gained + window(padded_portion, lane, extent_rows, extent_cols)
    return gained


def tally_volume(contribution, bubble, count):
    labels = jnp.arange(count, dtype=jnp.int32)
    layer_terms = contribution.reshape(contribution.shape[0], -1)
    layer_labels = bubble.reshape(bubble.shape[0], -1)

    def accumulate(running, layer_pair):
        terms, cell_labels = layer_pair
        indicator = (cell_labels[:, None] == labels[None, :]).astype(jnp.float32)
        summed = jnp.dot(
            terms, indicator, precision=lax.Precision.HIGHEST, preferred_element_type=jnp.float32
        )
        return (running + summed, None)

    running, _ = lax.scan(accumulate, jnp.zeros((count,), jnp.float32), (layer_terms, layer_labels))
    return running


def spread_density(gas_density, bubble):
    labels = jnp.arange(gas_density.shape[0], dtype=jnp.int32)
    layer_labels = bubble.reshape(bubble.shape[0], -1)

    def lookup(cell_labels):
        indicator = (cell_labels[:, None] == labels[None, :]).astype(jnp.float32)
        return jnp.dot(
            indicator,
            gas_density,
            precision=lax.Precision.HIGHEST,
            preferred_element_type=jnp.float32,
        )

    return lax.map(lookup, layer_labels).reshape(bubble.shape)


def total_volume(partial_volume):
    return lax.psum(partial_volume, ("gx", "gy"))


def shards(populations, cell_mass, cell_flags, bubble, conversion, rest_volume):
    extent_rows, extent_cols, extent_depth = (
        populations.shape[1],
        populations.shape[2],
        populations.shape[3],
    )
    density, velocity = moments(populations)
    fraction = jnp.clip(cell_mass / density, 0.0, 1.0)
    status = jnp.where((cell_flags == 1) & (conversion == 1), 4, cell_flags).astype(jnp.float32)
    contribution = jnp.where(cell_flags == 0, 1.0, jnp.where(cell_flags == 1, 1.0 - fraction, 0.0))
    partial_volume = tally_volume(contribution, bubble, rest_volume.shape[0])
    volume = total_volume(partial_volume)
    channels = jnp.concatenate([populations, fraction[None], status[None]], axis=0)
    padded = padded_2(channels, (("gx", 1), ("gy", 2)), 1)
    start_rows = lax.axis_index("gx") * extent_rows + jnp.arange(
        -1, extent_rows + 1, dtype=jnp.int32
    )
    start_cols = lax.axis_index("gy") * extent_cols + jnp.arange(
        -1, extent_cols + 1, dtype=jnp.int32
    )
    inside_rows = (start_rows >= 0) & (start_rows < extent_rows * lax.axis_size("gx"))
    inside_cols = (start_cols >= 0) & (start_cols < extent_cols * lax.axis_size("gy"))
    pulled, gas_side, mass_flux, targets = pull_cells(
        padded, inside_rows, inside_cols, populations, fraction
    )
    gas_density = AMBIENT + rest_volume / jnp.maximum(volume, 1.0)
    local_gas = spread_density(gas_density, bubble)
    relaxed, updated, portion = settle_cells(
        pulled,
        gas_side,
        populations,
        velocity,
        local_gas,
        cell_mass,
        cell_flags,
        conversion,
        mass_flux,
        targets,
    )
    padded_portion = padded_2(portion, (("gx", 0), ("gy", 1)), 1)
    gained = collect_spill(padded_portion, extent_rows, extent_cols)
    receiver = (cell_flags == 1) & (conversion == 0)
    new_mass = jnp.where(receiver, updated + gained, updated)
    return (relaxed, new_mass, gas_density)


def solution(mesh):
    placed = (
        P(None, "gx", "gy", None),
        P("gx", "gy", None),
        P("gx", "gy", None),
        P("gx", "gy", None),
        P("gx", "gy", None),
        P(),
    )
    return jax.shard_map(
        shards,
        mesh=mesh,
        in_specs=placed,
        out_specs=(P(None, "gx", "gy", None), P("gx", "gy", None), P()),
        check_vma=False,
    )
```

profile of v0, /device:TPU:9, one launch (start us, length us, event | category | flops | bytes accessed | tf_op | source)
XLA Modules:
  0.0 112.9 jit_solution(17620983186998840845)
XLA Ops:
  0.6 1.1 reduce_sum.36
  1.8 0.8 convert_bitcast_fusion
  2.6 3.1 %collective-permute-start = (f32[21,1,8,128]{3,2,1,0:T(8,128)S(1)}, f32[21,1,8,128]{3,2,1,0:T(8,128)S(1)}, u32[]{:S(2)}, u32[]{:S(2)}) collective-permute-start(f32[21,1,8,128]{3,2,1,0:T(8,128)S(1)} %get-tuple-element.136), channel_id=1, source_target_pairs={{0,4},{4,8},{8,12},{12,16},{16,20},{20,24},{24,28},{1,5},{5,9},{9,... | collective-permute-start | bytes 258056 | tf_op jit(solution)/shard_map/ppermute | solution.py:44
  5.7 3.1 %collective-permute-start.1 = (f32[21,1,8,128]{3,2,1,0:T(8,128)S(1)}, f32[21,1,8,128]{3,2,1,0:T(8,128)S(1)}, u32[]{:S(2)}, u32[]{:S(2)}) collective-permute-start(f32[21,1,8,128]{3,2,1,0:T(8,128)S(1)} %get-tuple-element.137), channel_id=1, source_target_pairs={{4,0},{8,4},{12,8},{16,12},{20,16},{24,20},{28,24},{5,1},{9,5},{13... | collective-permute-start | bytes 258056 | tf_op jit(solution)/shard_map/ppermute | solution.py:46
  11.7 0.8 fusion.15
  12.6 0.7 copy-done.58
  13.3 2.5 %while.23 = (s32[]{:T(128)}, f32[96]{0:T(128)S(1)}, f32[6,1024]{1,0:T(8,128)S(1)}, s32[6,1024]{1,0:T(8,128)S(1)}, s32[]{:T(128)}, /*index=5*/s32[]{:T(128)}) while((s32[]{:T(128)}, f32[96]{0:T(128)S(1)}, f32[6,1024]{1,0:T(8,128)S(1)}, s32[6,1024]{1,0:T(8,128)S(1)}, s32[]{:T(128)}, /*index=5*/s32[]{:T(128)}) %tuple.207), condition=%wide.region_2.3_spmd.clone, body=%wide.region_1.2_spmd.clone.sunk | while | flops 1278147 | bytes 17367 | solution.py:161
  15.8 39.3 %psum.7 = f32[96]{0:T(128)S(1)} all-reduce(f32[96]{0:T(128)S(1)} %get-tuple-element.57), channel_id=1, replica_groups=mesh['gx'=8,'gy'=4] {'gx','gy'}, use_global_device_ids=true, to_apply=%region_3.4 | all-reduce | flops 96 | bytes 768 | tf_op jit(solution)/shard_map/psum | solution.py:182
  55.1 3.5 %while.22 = (s32[]{:T(128)}, f32[6,1024]{1,0:T(8,128)S(1)}, s32[6,1024]{1,0:T(8,128)S(1)}, f32[96]{0:T(128)S(1)}, s32[]{:T(128)}, /*index=5*/s32[]{:T(128)}) while((s32[]{:T(128)}, f32[6,1024]{1,0:T(8,128)S(1)}, s32[6,1024]{1,0:T(8,128)S(1)}, f32[96]{0:T(128)S(1)}, s32[]{:T(128)}, /*index=5*/s32[]{:T(128)}) %tuple.206), condition=%wide.region_5.6_spmd.clone, body=%wide.region_4.5_spmd.clone.sunk | while | flops 1277954 | bytes 25037 | solution.py:178
  61.2 5.3 %collective-permute-start.2 = (f32[21,8,1,128]{3,2,1,0:T(1,128)S(1)}, f32[21,8,1,128]{3,2,1,0:T(1,128)S(1)}, u32[]{:S(2)}, u32[]{:S(2)}) collective-permute-start(f32[21,8,1,128]{3,2,1,0:T(1,128)S(1)} %get-tuple-element.132), channel_id=1, source_target_pairs={{0,1},{1,2},{2,3},{4,5},{5,6},{6,7},{8,9},{9,10},{10,11},{12,13},{... | collective-permute-start | bytes 258056 | tf_op jit(solution)/shard_map/ppermute | solution.py:44
  66.4 1.9 %collective-permute-start.3 = (f32[21,8,1,128]{3,2,1,0:T(1,128)S(1)}, f32[21,8,1,128]{3,2,1,0:T(1,128)S(1)}, u32[]{:S(2)}, u32[]{:S(2)}) collective-permute-start(f32[21,8,1,128]{3,2,1,0:T(1,128)S(1)} %get-tuple-element.133), channel_id=1, source_target_pairs={{1,0},{2,1},{3,2},{5,4},{6,5},{7,6},{9,8},{10,9},{11,10},{13,12},{... | collective-permute-start | bytes 258056 | tf_op jit(solution)/shard_map/ppermute | solution.py:46
  68.4 3.9 %collective-permute-done.3 = f32[21,8,1,128]{3,2,1,0:T(1,128)S(1)} collective-permute-done((f32[21,8,1,128]{3,2,1,0:T(1,128)S(1)}, f32[21,8,1,128]{3,2,1,0:T(1,128)S(1)}, u32[]{:S(2)}, u32[]{:S(2)}) %collective-permute-start.3) | collective-permute-done | bytes 86048 | tf_op jit(solution)/shard_map/ppermute | solution.py:46
  72.3 0.8 fusion.207
  73.0 0.8 fusion.208
  73.8 0.8 fusion.185
  74.6 0.7 fusion.186
  81.8 0.7 fusion.180
  82.6 0.7 bitcast_select_fusion.6
  85.5 0.7 bitcast_select_fusion
  86.2 0.8 maximum_select_fusion.4
  87.0 0.7 maximum_select_fusion.8
  87.7 3.1 %stack.91 = f32[19,6,8,128]{3,0,2,1:T(8,128)S(1)} concatenate(f32[1,6,8,128]{3,0,2,1:T(1,128)} %bitcast.312, f32[1,6,8,128]{3,0,2,1:T(1,128)} %bitcast.316, f32[1,6,8,128]{3,0,2,1:T(1,128)} %bitcast.315, f32[1,6,8,128]{3,0,2,1:T(1,128)} %bitcast.322, f32[1,6,8,128]{3,0,2,1:T(1,128)} %bitcast.321, f32[1,6,8,128]{3,0,2,1:T(1,128)} %bitcast.325, f32[1,6,8,128]{3,0,2,1:T(1,128)} %bitcast.326, ...), dimensions={0} | concatenate | bytes 933888 | tf_op jit(solution)/shard_map/stack | solution.py:108
  91.2 1.5 %fusion.178 = (f32[6,8,128]{2,1,0:T(8,128)S(1)}, f32[19,6,8,128]{3,0,2,1:T(8,128)S(1)}) fusion(f32[19,6,8,128]{3,2,1,0:T(8,128)S(1)} %copy-done, f32[19,6,8,128]{3,0,2,1:T(8,128)S(1)} %stack.91, f32[19,6,8,128]{3,2,1,0:T(8,128)S(1)} %gather_fusion.1, f32[19,6,8,128]{3,0,2,1:T(8,128)S(1)} %fusion.15, f32[19,6,8,128]{3,2,1,0:T(8,128)S(1)} %gather_fusion, ...), kind=kLoop, calls=%fused_computation.443 | loop fusion | flops 694272 | bytes 2973696 | tf_op jit(solution)/shard_map/reduce_sum | solution.py:54
  93.4 1.7 %divide_select_fusion = (f32[6,8,128]{2,1,0:T(8,128)S(1)}, f32[6,8,128]{2,1,0:T(8,128)S(1)}) fusion(f32[6,8,128]{2,1,0:T(8,128)S(1)} %get-tuple-element.110, f32[8,10,128]{2,1,0:T(8,128)S(1)} %get-tuple-element.114, pred[6,8]{1,0:T(8,128)(4,1)} %get-tuple-element.290, pred[6,8]{1,0:T(8,128)(4,1)} %get-tuple-element.284, ...), kind=kLoop, calls=%fused_computation.340 | loop fusion | flops 2463744 | bytes 1941936 | tf_op jit(solution)/shard_map/jit(_where)/select_n | solution.py:136
  95.1 3.1 %collective-permute-start.4 = (f32[1,8,128]{2,1,0:T(8,128)S(1)}, f32[1,8,128]{2,1,0:T(8,128)S(1)}, u32[]{:S(2)}, u32[]{:S(2)}) collective-permute-start(f32[1,8,128]{2,1,0:T(8,128)S(1)} %get-tuple-element.282), channel_id=1, source_target_pairs={{0,4},{4,8},{8,12},{12,16},{16,20},{20,24},{24,28},{1,5},{5,9},{9,... | collective-permute-start | bytes 12296 | tf_op jit(solution)/shard_map/ppermute | solution.py:44
  98.3 3.1 %collective-permute-start.5 = (f32[1,8,128]{2,1,0:T(8,128)S(1)}, f32[1,8,128]{2,1,0:T(8,128)S(1)}, u32[]{:S(2)}, u32[]{:S(2)}) collective-permute-start(f32[1,8,128]{2,1,0:T(8,128)S(1)} %get-tuple-element.283), channel_id=1, source_target_pairs={{4,0},{8,4},{12,8},{16,12},{20,16},{24,20},{28,24},{5,1},{9,5},{13... | collective-permute-start | bytes 12296 | tf_op jit(solution)/shard_map/ppermute | solution.py:46
  102.6 1.0 fusion.23
  103.6 0.9 copy.112
  104.4 2.4 %collective-permute-start.6 = (f32[8,1,128]{2,1,0:T(1,128)S(1)}, f32[8,1,128]{2,1,0:T(1,128)S(1)}, u32[]{:S(2)}, u32[]{:S(2)}) collective-permute-start(f32[8,1,128]{2,1,0:T(1,128)S(1)} %get-tuple-element.271), channel_id=1, source_target_pairs={{0,1},{1,2},{2,3},{4,5},{5,6},{6,7},{8,9},{9,10},{10,11},{12,13},{... | collective-permute-start | bytes 12296 | tf_op jit(solution)/shard_map/ppermute | solution.py:44
  106.9 1.9 %collective-permute-start.7 = (f32[8,1,128]{2,1,0:T(1,128)S(1)}, f32[8,1,128]{2,1,0:T(1,128)S(1)}, u32[]{:S(2)}, u32[]{:S(2)}) collective-permute-start(f32[8,1,128]{2,1,0:T(1,128)S(1)} %get-tuple-element.270), channel_id=1, source_target_pairs={{1,0},{2,1},{3,2},{5,4},{6,5},{7,6},{9,8},{10,9},{11,10},{13,12},{... | collective-permute-start | bytes 12296 | tf_op jit(solution)/shard_map/ppermute | solution.py:46
  109.0 2.8 %collective-permute-done.7 = f32[8,1,128]{2,1,0:T(1,128)S(1)} collective-permute-done((f32[8,1,128]{2,1,0:T(1,128)S(1)}, f32[8,1,128]{2,1,0:T(1,128)S(1)}, u32[]{:S(2)}, u32[]{:S(2)}) %collective-permute-start.7) | collective-permute-done | bytes 4128 | tf_op jit(solution)/shard_map/ppermute | solution.py:46
  112.1 0.8 add_select_fusion
  (254 shorter events, 21.9 us)
Async XLA Ops:
  0.6 2.0 %copy-start = (f32[19,6,8,128]{3,2,1,0:T(8,128)S(1)}, f32[19,6,8,128]{3,2,1,0:T(8,128)}, u32[]{:S(2)}) copy-start(f32[19,6,8,128]{3,2,1,0:T(8,128)} %param.19) | copy-start | bytes 1400836
  1.8 8.0 %copy-start.3 = (f32[6,8,128]{2,1,0:T(8,128)}, f32[6,8,128]{2,1,0:T(8,128)S(1)}, u32[]{:S(2)}) copy-start(f32[6,8,128]{2,1,0:T(8,128)S(1)} %reduce_sum.36) | copy-start | bytes 73732
  2.6 58.4 %collective-permute-start = (f32[21,1,8,128]{3,2,1,0:T(8,128)S(1)}, f32[21,1,8,128]{3,2,1,0:T(8,128)S(1)}, u32[]{:S(2)}, u32[]{:S(2)}) collective-permute-start(f32[21,1,8,128]{3,2,1,0:T(8,128)S(1)} %get-tuple-element.136), channel_id=1, source_target_pairs={{0,4},{4,8},{8,12},{12,16},{16,20},{20,24},{24,28},{1,5},{5,9},{9,... | collective-permute-start | bytes 258056 | tf_op jit(solution)/shard_map/ppermute | solution.py:44
  5.7 55.3 %collective-permute-start.1 = (f32[21,1,8,128]{3,2,1,0:T(8,128)S(1)}, f32[21,1,8,128]{3,2,1,0:T(8,128)S(1)}, u32[]{:S(2)}, u32[]{:S(2)}) collective-permute-start(f32[21,1,8,128]{3,2,1,0:T(8,128)S(1)} %get-tuple-element.137), channel_id=1, source_target_pairs={{4,0},{8,4},{12,8},{16,12},{20,16},{24,20},{28,24},{5,1},{9,5},{13... | collective-permute-start | bytes 258056 | tf_op jit(solution)/shard_map/ppermute | solution.py:46
  15.8 39.3 %copy-start.64 = (f32[96]{0:T(128)S(1)}, f32[96]{0:T(128)}, u32[]{:S(2)}) copy-start(f32[96]{0:T(128)} %param.24) | copy-start | bytes 1156
  61.2 7.2 %collective-permute-start.2 = (f32[21,8,1,128]{3,2,1,0:T(1,128)S(1)}, f32[21,8,1,128]{3,2,1,0:T(1,128)S(1)}, u32[]{:S(2)}, u32[]{:S(2)}) collective-permute-start(f32[21,8,1,128]{3,2,1,0:T(1,128)S(1)} %get-tuple-element.132), channel_id=1, source_target_pairs={{0,1},{1,2},{2,3},{4,5},{5,6},{6,7},{8,9},{9,10},{10,11},{12,13},{... | collective-permute-start | bytes 258056 | tf_op jit(solution)/shard_map/ppermute | solution.py:44
  66.4 5.8 %collective-permute-start.3 = (f32[21,8,1,128]{3,2,1,0:T(1,128)S(1)}, f32[21,8,1,128]{3,2,1,0:T(1,128)S(1)}, u32[]{:S(2)}, u32[]{:S(2)}) collective-permute-start(f32[21,8,1,128]{3,2,1,0:T(1,128)S(1)} %get-tuple-element.133), channel_id=1, source_target_pairs={{1,0},{2,1},{3,2},{5,4},{6,5},{7,6},{9,8},{10,9},{11,10},{13,12},{... | collective-permute-start | bytes 258056 | tf_op jit(solution)/shard_map/ppermute | solution.py:46
  87.7 3.1 %copy-start.14 = (pred[19,6,8,128]{3,2,1,0:T(8,128)(4,1)S(1)}, pred[19,6,8,128]{3,2,1,0:T(8,128)(4,1)}, u32[]{:S(2)}) copy-start(pred[19,6,8,128]{3,2,1,0:T(8,128)(4,1)} %copy-done.13) | copy-start | bytes 350212
  90.8 1.9 %copy-start.16 = (f32[6,8,1]{2,1,0:T(8,128)S(1)}, f32[6,8,1]{2,1,0:T(8,128)}, u32[]{:S(2)}) copy-start(f32[6,8,1]{2,1,0:T(8,128)} %get-tuple-element.239) | copy-start | bytes 580
  90.8 1.9 %copy-start.17 = (f32[6,8,1]{2,1,0:T(8,128)S(1)}, f32[6,8,1]{2,1,0:T(8,128)}, u32[]{:S(2)}) copy-start(f32[6,8,1]{2,1,0:T(8,128)} %get-tuple-element.240) | copy-start | bytes 580
  90.8 1.9 %copy-start.18 = (f32[6,8,1]{2,1,0:T(8,128)S(1)}, f32[6,8,1]{2,1,0:T(8,128)}, u32[]{:S(2)}) copy-start(f32[6,8,1]{2,1,0:T(8,128)} %get-tuple-element.241) | copy-start | bytes 580
  90.8 1.9 %copy-start.19 = (f32[6,8,1]{2,1,0:T(8,128)S(1)}, f32[6,8,1]{2,1,0:T(8,128)}, u32[]{:S(2)}) copy-start(f32[6,8,1]{2,1,0:T(8,128)} %get-tuple-element.242) | copy-start | bytes 580
  90.9 1.9 %copy-start.20 = (f32[6,8,1]{2,1,0:T(8,128)S(1)}, f32[6,8,1]{2,1,0:T(8,128)}, u32[]{:S(2)}) copy-start(f32[6,8,1]{2,1,0:T(8,128)} %get-tuple-element.243) | copy-start | bytes 580
  90.9 1.9 %copy-start.21 = (f32[6,8,1]{2,1,0:T(8,128)S(1)}, f32[6,8,1]{2,1,0:T(8,128)}, u32[]{:S(2)}) copy-start(f32[6,8,1]{2,1,0:T(8,128)} %get-tuple-element.244) | copy-start | bytes 580
  90.9 1.9 %copy-start.22 = (f32[6,8,1]{2,1,0:T(8,128)S(1)}, f32[6,8,1]{2,1,0:T(8,128)}, u32[]{:S(2)}) copy-start(f32[6,8,1]{2,1,0:T(8,128)} %get-tuple-element.245) | copy-start | bytes 580
  90.9 1.9 %copy-start.23 = (f32[6,8,1]{2,1,0:T(8,128)S(1)}, f32[6,8,1]{2,1,0:T(8,128)}, u32[]{:S(2)}) copy-start(f32[6,8,1]{2,1,0:T(8,128)} %get-tuple-element.246) | copy-start | bytes 580
  90.9 1.9 %copy-start.24 = (f32[6,8,127]{2,1,0:T(8,128)S(1)}, f32[6,8,127]{2,1,0:T(8,128)}, u32[]{:S(2)}) copy-start(f32[6,8,127]{2,1,0:T(8,128)} %get-tuple-element.247) | copy-start | bytes 73156
  90.9 1.9 %copy-start.25 = (f32[6,8,127]{2,1,0:T(8,128)S(1)}, f32[6,8,127]{2,1,0:T(8,128)}, u32[]{:S(2)}) copy-start(f32[6,8,127]{2,1,0:T(8,128)} %get-tuple-element.258) | copy-start | bytes 73156
  90.9 1.9 %copy-start.26 = (f32[6,8,127]{2,1,0:T(8,128)S(1)}, f32[6,8,127]{2,1,0:T(8,128)}, u32[]{:S(2)}) copy-start(f32[6,8,127]{2,1,0:T(8,128)} %get-tuple-element.259) | copy-start | bytes 73156
  90.9 1.9 %copy-start.27 = (f32[6,8,127]{2,1,0:T(8,128)S(1)}, f32[6,8,127]{2,1,0:T(8,128)}, u32[]{:S(2)}) copy-start(f32[6,8,127]{2,1,0:T(8,128)} %get-tuple-element.260) | copy-start | bytes 73156
  90.9 1.9 %copy-start.28 = (f32[6,8,127]{2,1,0:T(8,128)S(1)}, f32[6,8,127]{2,1,0:T(8,128)}, u32[]{:S(2)}) copy-start(f32[6,8,127]{2,1,0:T(8,128)} %get-tuple-element.261) | copy-start | bytes 73156
  90.9 1.9 %copy-start.29 = (f32[6,8,127]{2,1,0:T(8,128)S(1)}, f32[6,8,127]{2,1,0:T(8,128)}, u32[]{:S(2)}) copy-start(f32[6,8,127]{2,1,0:T(8,128)} %get-tuple-element.262) | copy-start | bytes 73156
  91.0 1.9 %copy-start.30 = (f32[6,8,127]{2,1,0:T(8,128)S(1)}, f32[6,8,127]{2,1,0:T(8,128)}, u32[]{:S(2)}) copy-start(f32[6,8,127]{2,1,0:T(8,128)} %get-tuple-element.263) | copy-start | bytes 73156
  91.0 1.9 %copy-start.31 = (f32[6,8,127]{2,1,0:T(8,128)S(1)}, f32[6,8,127]{2,1,0:T(8,128)}, u32[]{:S(2)}) copy-start(f32[6,8,127]{2,1,0:T(8,128)} %get-tuple-element.264) | copy-start | bytes 73156
  91.0 1.9 %copy-start.32 = (f32[6,8,127]{2,1,0:T(8,128)S(1)}, f32[6,8,127]{2,1,0:T(8,128)}, u32[]{:S(2)}) copy-start(f32[6,8,127]{2,1,0:T(8,128)} %get-tuple-element.265) | copy-start | bytes 73156
  91.0 1.9 %copy-start.33 = (f32[6,8,1]{2,1,0:T(8,128)S(1)}, f32[6,8,1]{2,1,0:T(8,128)}, u32[]{:S(2)}) copy-start(f32[6,8,1]{2,1,0:T(8,128)} %get-tuple-element.168) | copy-start | bytes 580
  91.0 1.9 %copy-start.34 = (f32[6,8,1]{2,1,0:T(8,128)S(1)}, f32[6,8,1]{2,1,0:T(8,128)}, u32[]{:S(2)}) copy-start(f32[6,8,1]{2,1,0:T(8,128)} %get-tuple-element.169) | copy-start | bytes 580
  95.1 6.2 %copy-start.69 = (f32[3,19,1,1]{1,0,3,2:T(4,128)S(1)}, f32[3,19,1,1]{1,0,3,2:T(4,128)}, u32[]{:S(2)}) copy-start(f32[3,19,1,1]{1,0,3,2:T(4,128)} %constant.139) | copy-start | bytes 688
  95.1 9.3 %collective-permute-start.4 = (f32[1,8,128]{2,1,0:T(8,128)S(1)}, f32[1,8,128]{2,1,0:T(8,128)S(1)}, u32[]{:S(2)}, u32[]{:S(2)}) collective-permute-start(f32[1,8,128]{2,1,0:T(8,128)S(1)} %get-tuple-element.282), channel_id=1, source_target_pairs={{0,4},{4,8},{8,12},{12,16},{16,20},{20,24},{24,28},{1,5},{5,9},{9,... | collective-permute-start | bytes 12296 | tf_op jit(solution)/shard_map/ppermute | solution.py:44
  98.3 6.2 %collective-permute-start.5 = (f32[1,8,128]{2,1,0:T(8,128)S(1)}, f32[1,8,128]{2,1,0:T(8,128)S(1)}, u32[]{:S(2)}, u32[]{:S(2)}) collective-permute-start(f32[1,8,128]{2,1,0:T(8,128)S(1)} %get-tuple-element.283), channel_id=1, source_target_pairs={{4,0},{8,4},{12,8},{16,12},{20,16},{24,20},{28,24},{5,1},{9,5},{13... | collective-permute-start | bytes 12296 | tf_op jit(solution)/shard_map/ppermute | solution.py:46
  104.4 4.5 %collective-permute-start.6 = (f32[8,1,128]{2,1,0:T(1,128)S(1)}, f32[8,1,128]{2,1,0:T(1,128)S(1)}, u32[]{:S(2)}, u32[]{:S(2)}) collective-permute-start(f32[8,1,128]{2,1,0:T(1,128)S(1)} %get-tuple-element.271), channel_id=1, source_target_pairs={{0,1},{1,2},{2,3},{4,5},{5,6},{6,7},{8,9},{9,10},{10,11},{12,13},{... | collective-permute-start | bytes 12296 | tf_op jit(solution)/shard_map/ppermute | solution.py:44
  106.9 4.9 %collective-permute-start.7 = (f32[8,1,128]{2,1,0:T(1,128)S(1)}, f32[8,1,128]{2,1,0:T(1,128)S(1)}, u32[]{:S(2)}, u32[]{:S(2)}) collective-permute-start(f32[8,1,128]{2,1,0:T(1,128)S(1)} %get-tuple-element.270), channel_id=1, source_target_pairs={{1,0},{2,1},{3,2},{5,4},{6,5},{7,6},{9,8},{10,9},{11,10},{13,12},{... | collective-permute-start | bytes 12296 | tf_op jit(solution)/shard_map/ppermute | solution.py:46
  (48 other events, 54.5 us)
where the time goes:
time: 114 us; the launch traced here: 113 us
  blocking collectives  39.3 us (34%)
  starting transfers between devices  23.9 us (21%)
  local copies, waits for them, and re-layouts  19.9 us (17%)
  other arithmetic  13 us (11%)
  matrix products  7.83 us (7%)
  waiting for transfers between devices  6.69 us (6%)
  between operations  1.85 us (2%)
    psum x1, blocking collectives, total_volume(): return lax.psum(partial_volume, ('gx', 'gy'))  39.3 us
    ppermute x4, starting transfers between devices, padded_2(): lax.ppermute(tail, axis, [(i, (i + 1) % count) for i in range(ends)])  13.9 us
    unnamed x150, local copies, waits for them, and re-layouts  10.6 us
    ppermute x4, starting transfers between devices, padded_2(): lax.ppermute(head, axis, [((i + 1) % count, i) for i in range(ends)])  9.98 us
    ppermute x4, waiting for transfers between devices, padded_2(): lax.ppermute(head, axis, [((i + 1) % count, i) for i in range(ends)])  6.68 us
    slice x20, local copies, waits for them, and re-layouts, window(): jnp.roll(layer[begin_rows:begin_rows + extent_rows, begin_cols:begin_cols...  4.09 us
    another operation x1, local copies, waits for them, and re-layouts, pull_cells(): return (jnp.stack(pulled), jnp.stack(gas_side), mass_flux, targets)  3.12 us
    select_n x4, other arithmetic, pull_cells(): pulled.append(jnp.where(in_domain, source, bounced))  2.9 us
  transfers between devices with their start and end apart: 8, of which 2 were waited for; matrix products, arithmetic and copies ran while one was open for 11% of the time, Pallas kernels for 0%

commit v1 on v0

--- a/solution.py
+++ b/solution.py
@@ -179,7 +179,7 @@
 
 
 def total_volume(partial_volume):
-    return lax.psum(partial_volume, ("gx", "gy"))
+    return jnp.sum(lax.all_gather(partial_volume, ("gx", "gy")), axis=0)
 
 
 def shards(populations, cell_mass, cell_flags, bubble, conversion, rest_volume):

time: 114 us -> 118 us (1.035)
  local copies, waits for them, and re-layouts: 19.9 us -> 23.9 us
    unnamed x0 -> x1, blocking collectives: none -> 39.4 us
    psum x1 -> x0, blocking collectives: 39.3 us -> none  [total_volume(): return lax.psum(partial_volume, ('gx', 'gy'))]
    slice x20, local copies, waits for them, and re-layouts: 4.09 us -> 7.1 us  [window(): jnp.roll(layer[begin_rows:begin_rows + extent_rows, begin_cols:begin_cols...]
    unnamed x150 -> x154, local copies, waits for them, and re-layouts: 10.6 us -> 11.6 us
where the time goes in v1:
time: 118 us; the launch traced here: 117 us
  blocking collectives  39.4 us (33%)
  local copies, waits for them, and re-layouts  23.9 us (20%)
  starting transfers between devices  23.9 us (20%)
  other arithmetic  12.6 us (11%)
  matrix products  7.83 us (7%)
  waiting for transfers between devices  6.69 us (6%)
  between operations  1.89 us (2%)
    unnamed x1, blocking collectives  39.4 us
    ppermute x4, starting transfers between devices, padded_2(): lax.ppermute(tail, axis, [(i, (i + 1) % count) for i in range(ends)])  13.9 us
    unnamed x154, local copies, waits for them, and re-layouts  11.6 us
    ppermute x4, starting transfers between devices, padded_2(): lax.ppermute(head, axis, [((i + 1) % count, i) for i in range(ends)])  9.98 us
    slice x20, local copies, waits for them, and re-layouts, window(): jnp.roll(layer[begin_rows:begin_rows + extent_rows, begin_cols:begin_cols...  7.1 us
    ppermute x4, waiting for transfers between devices, padded_2(): lax.ppermute(head, axis, [((i + 1) % count, i) for i in range(ends)])  6.68 us
    another operation x1, local copies, waits for them, and re-layouts, pull_cells(): return (jnp.stack(pulled), jnp.stack(gas_side), mass_flux, targets)  3.03 us
    dot_general x6, matrix products, lookup(): jnp.dot(indicator, gas_density, precision=lax.Precision.HIGHEST, preferre...  2.66 us
  transfers between devices with their start and end apart: 8, of which 2 were waited for; matrix products, arithmetic and copies ran while one was open for 11% of the time, Pallas kernels for 0%

profile of v1, /device:TPU:9, one launch (start us, length us, event | category | flops | bytes accessed | tf_op | source)
XLA Modules:
  0.0 116.5 jit_solution(7284970047253422985)
XLA Ops:
  0.6 1.1 reduce_sum.45
  1.8 0.8 convert_bitcast_fusion
  2.6 3.1 %collective-permute-start = (f32[21,1,8,128]{3,2,1,0:T(8,128)S(1)}, f32[21,1,8,128]{3,2,1,0:T(8,128)S(1)}, u32[]{:S(2)}, u32[]{:S(2)}) collective-permute-start(f32[21,1,8,128]{3,2,1,0:T(8,128)S(1)} %get-tuple-element.139), channel_id=1, source_target_pairs={{0,4},{4,8},{8,12},{12,16},{16,20},{20,24},{24,28},{1,5},{5,9},{9,... | collective-permute-start | bytes 258056 | tf_op jit(solution)/shard_map/ppermute | solution.py:44
  5.7 3.1 %collective-permute-start.1 = (f32[21,1,8,128]{3,2,1,0:T(8,128)S(1)}, f32[21,1,8,128]{3,2,1,0:T(8,128)S(1)}, u32[]{:S(2)}, u32[]{:S(2)}) collective-permute-start(f32[21,1,8,128]{3,2,1,0:T(8,128)S(1)} %get-tuple-element.140), channel_id=1, source_target_pairs={{4,0},{8,4},{12,8},{16,12},{20,16},{24,20},{28,24},{5,1},{9,5},{13... | collective-permute-start | bytes 258056 | tf_op jit(solution)/shard_map/ppermute | solution.py:46
  11.7 0.8 fusion.15
  12.6 0.7 copy-done.59
  13.3 2.5 %while.23 = (s32[]{:T(128)}, f32[96]{0:T(128)S(1)}, f32[6,1024]{1,0:T(8,128)S(1)}, s32[6,1024]{1,0:T(8,128)S(1)}, s32[]{:T(128)}, /*index=5*/s32[]{:T(128)}) while((s32[]{:T(128)}, f32[96]{0:T(128)S(1)}, f32[6,1024]{1,0:T(8,128)S(1)}, s32[6,1024]{1,0:T(8,128)S(1)}, s32[]{:T(128)}, /*index=5*/s32[]{:T(128)}) %tuple.208), condition=%wide.region_2.3_spmd.clone, body=%wide.region_1.2_spmd.clone.sunk | while | flops 1278147 | bytes 17367 | solution.py:161
  16.1 39.4 %all-reduce = f32[3072]{0:T(1024)S(1)} all-reduce(f32[3072]{0:T(1024)S(1)} %dynamic-update-slice), channel_id=2, replica_groups=mesh['gx'=8,'gy'=4] {'gx','gy'}, use_global_device_ids=true, to_apply=%add | all-reduce | flops 3072 | bytes 24576
  56.2 3.5 %while.22 = (s32[]{:T(128)}, f32[6,1024]{1,0:T(8,128)S(1)}, s32[6,1024]{1,0:T(8,128)S(1)}, f32[96]{0:T(128)S(1)}, s32[]{:T(128)}, /*index=5*/s32[]{:T(128)}) while((s32[]{:T(128)}, f32[6,1024]{1,0:T(8,128)S(1)}, s32[6,1024]{1,0:T(8,128)S(1)}, f32[96]{0:T(128)S(1)}, s32[]{:T(128)}, /*index=5*/s32[]{:T(128)}) %tuple.207), condition=%wide.region_5.6_spmd.clone, body=%wide.region_4.5_spmd.clone.sunk | while | flops 1277954 | bytes 25037 | solution.py:178
  62.3 5.3 %collective-permute-start.2 = (f32[21,8,1,128]{3,2,1,0:T(1,128)S(1)}, f32[21,8,1,128]{3,2,1,0:T(1,128)S(1)}, u32[]{:S(2)}, u32[]{:S(2)}) collective-permute-start(f32[21,8,1,128]{3,2,1,0:T(1,128)S(1)} %get-tuple-element.135), channel_id=1, source_target_pairs={{0,1},{1,2},{2,3},{4,5},{5,6},{6,7},{8,9},{9,10},{10,11},{12,13},{... | collective-permute-start | bytes 258056 | tf_op jit(solution)/shard_map/ppermute | solution.py:44
  67.6 1.9 %collective-permute-start.3 = (f32[21,8,1,128]{3,2,1,0:T(1,128)S(1)}, f32[21,8,1,128]{3,2,1,0:T(1,128)S(1)}, u32[]{:S(2)}, u32[]{:S(2)}) collective-permute-start(f32[21,8,1,128]{3,2,1,0:T(1,128)S(1)} %get-tuple-element.136), channel_id=1, source_target_pairs={{1,0},{2,1},{3,2},{5,4},{6,5},{7,6},{9,8},{10,9},{11,10},{13,12},{... | collective-permute-start | bytes 258056 | tf_op jit(solution)/shard_map/ppermute | solution.py:46
  69.5 3.9 %collective-permute-done.3 = f32[21,8,1,128]{3,2,1,0:T(1,128)S(1)} collective-permute-done((f32[21,8,1,128]{3,2,1,0:T(1,128)S(1)}, f32[21,8,1,128]{3,2,1,0:T(1,128)S(1)}, u32[]{:S(2)}, u32[]{:S(2)}) %collective-permute-start.3) | collective-permute-done | bytes 86048 | tf_op jit(solution)/shard_map/ppermute | solution.py:46
  73.4 0.8 fusion.207
  74.2 0.8 fusion.208
  75.0 0.8 fusion.185
  75.7 0.7 fusion.186
  85.3 0.7 fusion.180
  86.1 0.7 bitcast_select_fusion.6
  88.9 0.7 bitcast_select_fusion
  89.7 0.8 maximum_select_fusion.4
  90.6 0.7 copy-done.54
  91.3 3.0 %stack.91 = f32[19,6,8,128]{3,0,2,1:T(8,128)S(1)} concatenate(f32[1,6,8,128]{3,0,2,1:T(1,128)S(1)} %bitcast.312, f32[1,6,8,128]{3,0,2,1:T(1,128)S(1)} %bitcast.316, f32[1,6,8,128]{3,0,2,1:T(1,128)S(1)} %bitcast.315, f32[1,6,8,128]{3,0,2,1:T(1,128)} %bitcast.322, f32[1,6,8,128]{3,0,2,1:T(1,128)} %bitcast.321, f32[1,6,8,128]{3,0,2,1:T(1,128)} %bitcast.325, ...), dimensions={0} | concatenate | bytes 933888 | tf_op jit(solution)/shard_map/stack | solution.py:108
  94.7 1.5 %fusion.178 = (f32[6,8,128]{2,1,0:T(8,128)S(1)}, f32[19,6,8,128]{3,0,2,1:T(8,128)S(1)}) fusion(f32[19,6,8,128]{3,2,1,0:T(8,128)S(1)} %copy-done, f32[19,6,8,128]{3,0,2,1:T(8,128)S(1)} %stack.91, f32[19,6,8,128]{3,2,1,0:T(8,128)S(1)} %gather_fusion.1, f32[19,6,8,128]{3,0,2,1:T(8,128)S(1)} %fusion.15, f32[19,6,8,128]{3,2,1,0:T(8,128)S(1)} %gather_fusion, ...), kind=kLoop, calls=%fused_computation.443 | loop fusion | flops 694272 | bytes 2973696 | tf_op jit(solution)/shard_map/reduce_sum | solution.py:54
  97.0 1.8 %divide_select_fusion = (f32[6,8,128]{2,1,0:T(8,128)S(1)}, f32[6,8,128]{2,1,0:T(8,128)S(1)}) fusion(f32[6,8,128]{2,1,0:T(8,128)S(1)} %get-tuple-element.113, f32[8,10,128]{2,1,0:T(8,128)S(1)} %get-tuple-element.117, pred[6,8]{1,0:T(8,128)(4,1)} %get-tuple-element.293, pred[6,8]{1,0:T(8,128)(4,1)} %get-tuple-element.287, ...), kind=kLoop, calls=%fused_computation.340 | loop fusion | flops 2463744 | bytes 1941936 | tf_op jit(solution)/shard_map/jit(_where)/select_n | solution.py:136
  98.8 3.1 %collective-permute-start.4 = (f32[1,8,128]{2,1,0:T(8,128)S(1)}, f32[1,8,128]{2,1,0:T(8,128)S(1)}, u32[]{:S(2)}, u32[]{:S(2)}) collective-permute-start(f32[1,8,128]{2,1,0:T(8,128)S(1)} %get-tuple-element.285), channel_id=1, source_target_pairs={{0,4},{4,8},{8,12},{12,16},{16,20},{20,24},{24,28},{1,5},{5,9},{9,... | collective-permute-start | bytes 12296 | tf_op jit(solution)/shard_map/ppermute | solution.py:44
  101.9 3.1 %collective-permute-start.5 = (f32[1,8,128]{2,1,0:T(8,128)S(1)}, f32[1,8,128]{2,1,0:T(8,128)S(1)}, u32[]{:S(2)}, u32[]{:S(2)}) collective-permute-start(f32[1,8,128]{2,1,0:T(8,128)S(1)} %get-tuple-element.286), channel_id=1, source_target_pairs={{4,0},{8,4},{12,8},{16,12},{20,16},{24,20},{28,24},{5,1},{9,5},{13... | collective-permute-start | bytes 12296 | tf_op jit(solution)/shard_map/ppermute | solution.py:46
  106.2 1.0 fusion.23
  107.2 0.9 copy.161
  108.1 2.4 %collective-permute-start.6 = (f32[8,1,128]{2,1,0:T(1,128)S(1)}, f32[8,1,128]{2,1,0:T(1,128)S(1)}, u32[]{:S(2)}, u32[]{:S(2)}) collective-permute-start(f32[8,1,128]{2,1,0:T(1,128)S(1)} %get-tuple-element.274), channel_id=1, source_target_pairs={{0,1},{1,2},{2,3},{4,5},{5,6},{6,7},{8,9},{9,10},{10,11},{12,13},{... | collective-permute-start | bytes 12296 | tf_op jit(solution)/shard_map/ppermute | solution.py:44
  110.5 1.9 %collective-permute-start.7 = (f32[8,1,128]{2,1,0:T(1,128)S(1)}, f32[8,1,128]{2,1,0:T(1,128)S(1)}, u32[]{:S(2)}, u32[]{:S(2)}) collective-permute-start(f32[8,1,128]{2,1,0:T(1,128)S(1)} %get-tuple-element.273), channel_id=1, source_target_pairs={{1,0},{2,1},{3,2},{5,4},{6,5},{7,6},{9,8},{10,9},{11,10},{13,12},{... | collective-permute-start | bytes 12296 | tf_op jit(solution)/shard_map/ppermute | solution.py:46
  112.6 2.8 %collective-permute-done.7 = f32[8,1,128]{2,1,0:T(1,128)S(1)} collective-permute-done((f32[8,1,128]{2,1,0:T(1,128)S(1)}, f32[8,1,128]{2,1,0:T(1,128)S(1)}, u32[]{:S(2)}, u32[]{:S(2)}) %collective-permute-start.7) | collective-permute-done | bytes 4128 | tf_op jit(solution)/shard_map/ppermute | solution.py:46
  115.7 0.8 add_select_fusion
  (260 shorter events, 25.4 us)
Async XLA Ops:
  0.6 2.0 %copy-start = (f32[19,6,8,128]{3,2,1,0:T(8,128)S(1)}, f32[19,6,8,128]{3,2,1,0:T(8,128)}, u32[]{:S(2)}) copy-start(f32[19,6,8,128]{3,2,1,0:T(8,128)} %param.19) | copy-start | bytes 1400836
  1.8 8.0 %copy-start.3 = (f32[6,8,128]{2,1,0:T(8,128)}, f32[6,8,128]{2,1,0:T(8,128)S(1)}, u32[]{:S(2)}) copy-start(f32[6,8,128]{2,1,0:T(8,128)S(1)} %reduce_sum.45) | copy-start | bytes 73732
  2.6 59.5 %collective-permute-start = (f32[21,1,8,128]{3,2,1,0:T(8,128)S(1)}, f32[21,1,8,128]{3,2,1,0:T(8,128)S(1)}, u32[]{:S(2)}, u32[]{:S(2)}) collective-permute-start(f32[21,1,8,128]{3,2,1,0:T(8,128)S(1)} %get-tuple-element.139), channel_id=1, source_target_pairs={{0,4},{4,8},{8,12},{12,16},{16,20},{20,24},{24,28},{1,5},{5,9},{9,... | collective-permute-start | bytes 258056 | tf_op jit(solution)/shard_map/ppermute | solution.py:44
  5.7 56.4 %collective-permute-start.1 = (f32[21,1,8,128]{3,2,1,0:T(8,128)S(1)}, f32[21,1,8,128]{3,2,1,0:T(8,128)S(1)}, u32[]{:S(2)}, u32[]{:S(2)}) collective-permute-start(f32[21,1,8,128]{3,2,1,0:T(8,128)S(1)} %get-tuple-element.140), channel_id=1, source_target_pairs={{4,0},{8,4},{12,8},{16,12},{20,16},{24,20},{28,24},{5,1},{9,5},{13... | collective-permute-start | bytes 258056 | tf_op jit(solution)/shard_map/ppermute | solution.py:46
  62.3 7.2 %collective-permute-start.2 = (f32[21,8,1,128]{3,2,1,0:T(1,128)S(1)}, f32[21,8,1,128]{3,2,1,0:T(1,128)S(1)}, u32[]{:S(2)}, u32[]{:S(2)}) collective-permute-start(f32[21,8,1,128]{3,2,1,0:T(1,128)S(1)} %get-tuple-element.135), channel_id=1, source_target_pairs={{0,1},{1,2},{2,3},{4,5},{5,6},{6,7},{8,9},{9,10},{10,11},{12,13},{... | collective-permute-start | bytes 258056 | tf_op jit(solution)/shard_map/ppermute | solution.py:44
  67.6 5.8 %collective-permute-start.3 = (f32[21,8,1,128]{3,2,1,0:T(1,128)S(1)}, f32[21,8,1,128]{3,2,1,0:T(1,128)S(1)}, u32[]{:S(2)}, u32[]{:S(2)}) collective-permute-start(f32[21,8,1,128]{3,2,1,0:T(1,128)S(1)} %get-tuple-element.136), channel_id=1, source_target_pairs={{1,0},{2,1},{3,2},{5,4},{6,5},{7,6},{9,8},{10,9},{11,10},{13,12},{... | collective-permute-start | bytes 258056 | tf_op jit(solution)/shard_map/ppermute | solution.py:46
  91.3 3.0 %copy-start.14 = (pred[19,6,8,128]{3,2,1,0:T(8,128)(4,1)S(1)}, pred[19,6,8,128]{3,2,1,0:T(8,128)(4,1)}, u32[]{:S(2)}) copy-start(pred[19,6,8,128]{3,2,1,0:T(8,128)(4,1)} %copy-done.13) | copy-start | bytes 350212
  94.4 1.9 %copy-start.16 = (f32[6,8,1]{2,1,0:T(8,128)S(1)}, f32[6,8,1]{2,1,0:T(8,128)}, u32[]{:S(2)}) copy-start(f32[6,8,1]{2,1,0:T(8,128)} %get-tuple-element.242) | copy-start | bytes 580
  94.4 1.9 %copy-start.17 = (f32[6,8,1]{2,1,0:T(8,128)S(1)}, f32[6,8,1]{2,1,0:T(8,128)}, u32[]{:S(2)}) copy-start(f32[6,8,1]{2,1,0:T(8,128)} %get-tuple-element.243) | copy-start | bytes 580
  94.4 1.9 %copy-start.18 = (f32[6,8,1]{2,1,0:T(8,128)S(1)}, f32[6,8,1]{2,1,0:T(8,128)}, u32[]{:S(2)}) copy-start(f32[6,8,1]{2,1,0:T(8,128)} %get-tuple-element.244) | copy-start | bytes 580
  94.4 1.9 %copy-start.19 = (f32[6,8,1]{2,1,0:T(8,128)S(1)}, f32[6,8,1]{2,1,0:T(8,128)}, u32[]{:S(2)}) copy-start(f32[6,8,1]{2,1,0:T(8,128)} %get-tuple-element.245) | copy-start | bytes 580
  94.4 1.9 %copy-start.20 = (f32[6,8,1]{2,1,0:T(8,128)S(1)}, f32[6,8,1]{2,1,0:T(8,128)}, u32[]{:S(2)}) copy-start(f32[6,8,1]{2,1,0:T(8,128)} %get-tuple-element.246) | copy-start | bytes 580
  94.4 1.9 %copy-start.21 = (f32[6,8,1]{2,1,0:T(8,128)S(1)}, f32[6,8,1]{2,1,0:T(8,128)}, u32[]{:S(2)}) copy-start(f32[6,8,1]{2,1,0:T(8,128)} %get-tuple-element.247) | copy-start | bytes 580
  94.4 1.9 %copy-start.22 = (f32[6,8,1]{2,1,0:T(8,128)S(1)}, f32[6,8,1]{2,1,0:T(8,128)}, u32[]{:S(2)}) copy-start(f32[6,8,1]{2,1,0:T(8,128)} %get-tuple-element.248) | copy-start | bytes 580
  94.4 1.9 %copy-start.23 = (f32[6,8,1]{2,1,0:T(8,128)S(1)}, f32[6,8,1]{2,1,0:T(8,128)}, u32[]{:S(2)}) copy-start(f32[6,8,1]{2,1,0:T(8,128)} %get-tuple-element.249) | copy-start | bytes 580
  94.4 1.9 %copy-start.24 = (f32[6,8,127]{2,1,0:T(8,128)S(1)}, f32[6,8,127]{2,1,0:T(8,128)}, u32[]{:S(2)}) copy-start(f32[6,8,127]{2,1,0:T(8,128)} %get-tuple-element.250) | copy-start | bytes 73156
  94.5 1.9 %copy-start.25 = (f32[6,8,127]{2,1,0:T(8,128)S(1)}, f32[6,8,127]{2,1,0:T(8,128)}, u32[]{:S(2)}) copy-start(f32[6,8,127]{2,1,0:T(8,128)} %get-tuple-element.261) | copy-start | bytes 73156
  94.5 1.9 %copy-start.26 = (f32[6,8,127]{2,1,0:T(8,128)S(1)}, f32[6,8,127]{2,1,0:T(8,128)}, u32[]{:S(2)}) copy-start(f32[6,8,127]{2,1,0:T(8,128)} %get-tuple-element.262) | copy-start | bytes 73156
  94.5 1.9 %copy-start.27 = (f32[6,8,127]{2,1,0:T(8,128)S(1)}, f32[6,8,127]{2,1,0:T(8,128)}, u32[]{:S(2)}) copy-start(f32[6,8,127]{2,1,0:T(8,128)} %get-tuple-element.263) | copy-start | bytes 73156
  94.5 1.9 %copy-start.28 = (f32[6,8,127]{2,1,0:T(8,128)S(1)}, f32[6,8,127]{2,1,0:T(8,128)}, u32[]{:S(2)}) copy-start(f32[6,8,127]{2,1,0:T(8,128)} %get-tuple-element.264) | copy-start | bytes 73156
  94.5 1.9 %copy-start.29 = (f32[6,8,127]{2,1,0:T(8,128)S(1)}, f32[6,8,127]{2,1,0:T(8,128)}, u32[]{:S(2)}) copy-start(f32[6,8,127]{2,1,0:T(8,128)} %get-tuple-element.265) | copy-start | bytes 73156
  94.5 1.9 %copy-start.30 = (f32[6,8,127]{2,1,0:T(8,128)S(1)}, f32[6,8,127]{2,1,0:T(8,128)}, u32[]{:S(2)}) copy-start(f32[6,8,127]{2,1,0:T(8,128)} %get-tuple-element.266) | copy-start | bytes 73156
  94.5 1.9 %copy-start.31 = (f32[6,8,127]{2,1,0:T(8,128)S(1)}, f32[6,8,127]{2,1,0:T(8,128)}, u32[]{:S(2)}) copy-start(f32[6,8,127]{2,1,0:T(8,128)} %get-tuple-element.267) | copy-start | bytes 73156
  94.5 1.9 %copy-start.32 = (f32[6,8,127]{2,1,0:T(8,128)S(1)}, f32[6,8,127]{2,1,0:T(8,128)}, u32[]{:S(2)}) copy-start(f32[6,8,127]{2,1,0:T(8,128)} %get-tuple-element.268) | copy-start | bytes 73156
  94.5 1.9 %copy-start.33 = (f32[6,8,1]{2,1,0:T(8,128)S(1)}, f32[6,8,1]{2,1,0:T(8,128)}, u32[]{:S(2)}) copy-start(f32[6,8,1]{2,1,0:T(8,128)} %get-tuple-element.171) | copy-start | bytes 580
  94.5 1.9 %copy-start.34 = (f32[6,8,1]{2,1,0:T(8,128)S(1)}, f32[6,8,1]{2,1,0:T(8,128)}, u32[]{:S(2)}) copy-start(f32[6,8,1]{2,1,0:T(8,128)} %get-tuple-element.172) | copy-start | bytes 580
  94.6 1.9 %copy-start.35 = (f32[6,8,1]{2,1,0:T(8,128)S(1)}, f32[6,8,1]{2,1,0:T(8,128)}, u32[]{:S(2)}) copy-start(f32[6,8,1]{2,1,0:T(8,128)} %get-tuple-element.173) | copy-start | bytes 580
  98.8 6.2 %copy-start.70 = (f32[3,19,1,1]{1,0,3,2:T(4,128)S(1)}, f32[3,19,1,1]{1,0,3,2:T(4,128)}, u32[]{:S(2)}) copy-start(f32[3,19,1,1]{1,0,3,2:T(4,128)} %constant.143) | copy-start | bytes 688
  98.8 9.3 %collective-permute-start.4 = (f32[1,8,128]{2,1,0:T(8,128)S(1)}, f32[1,8,128]{2,1,0:T(8,128)S(1)}, u32[]{:S(2)}, u32[]{:S(2)}) collective-permute-start(f32[1,8,128]{2,1,0:T(8,128)S(1)} %get-tuple-element.285), channel_id=1, source_target_pairs={{0,4},{4,8},{8,12},{12,16},{16,20},{20,24},{24,28},{1,5},{5,9},{9,... | collective-permute-start | bytes 12296 | tf_op jit(solution)/shard_map/ppermute | solution.py:44
  101.9 6.2 %collective-permute-start.5 = (f32[1,8,128]{2,1,0:T(8,128)S(1)}, f32[1,8,128]{2,1,0:T(8,128)S(1)}, u32[]{:S(2)}, u32[]{:S(2)}) collective-permute-start(f32[1,8,128]{2,1,0:T(8,128)S(1)} %get-tuple-element.286), channel_id=1, source_target_pairs={{4,0},{8,4},{12,8},{16,12},{20,16},{24,20},{28,24},{5,1},{9,5},{13... | collective-permute-start | bytes 12296 | tf_op jit(solution)/shard_map/ppermute | solution.py:46
  108.1 4.5 %collective-permute-start.6 = (f32[8,1,128]{2,1,0:T(1,128)S(1)}, f32[8,1,128]{2,1,0:T(1,128)S(1)}, u32[]{:S(2)}, u32[]{:S(2)}) collective-permute-start(f32[8,1,128]{2,1,0:T(1,128)S(1)} %get-tuple-element.274), channel_id=1, source_target_pairs={{0,1},{1,2},{2,3},{4,5},{5,6},{6,7},{8,9},{9,10},{10,11},{12,13},{... | collective-permute-start | bytes 12296 | tf_op jit(solution)/shard_map/ppermute | solution.py:44
  110.5 4.9 %collective-permute-start.7 = (f32[8,1,128]{2,1,0:T(1,128)S(1)}, f32[8,1,128]{2,1,0:T(1,128)S(1)}, u32[]{:S(2)}, u32[]{:S(2)}) collective-permute-start(f32[8,1,128]{2,1,0:T(1,128)S(1)} %get-tuple-element.273), channel_id=1, source_target_pairs={{1,0},{2,1},{3,2},{5,4},{6,5},{7,6},{9,8},{10,9},{11,10},{13,12},{... | collective-permute-start | bytes 12296 | tf_op jit(solution)/shard_map/ppermute | solution.py:46
  (49 other events, 54.8 us)
